TPU v7x, 32 devices: a whole 2x2x4 slice. The times are simulated.
32 devices in a mesh: dom: 32 (over z, y, x, core).
Axes of the slice: x: 2, y: 2, z: 4, core: 2. Of those that a mesh axis runs over, the one named last changes fastest.
Arguments:
- features: bfloat16 [131072, 256], P('dom'), may hold values from -6 to 6
- weight: bfloat16 [256, 256], replicated, may hold values from -0.375 to 0.375
- bias_vector: float32 [256], replicated, may hold values from -3 to 3
- tile_values: bfloat16 [8192, 128, 128], P('dom'), may hold values from -0.1875 to 0.1875
- tile_row: int32 [32, 256], P('dom'), may hold values from 0 to 31
- tile_col: int32 [32, 256], P('dom'), may hold values from 0 to 35
- tile_count: int32 [32], P('dom'), may hold values from 64 to 256, as said below
- send_rows: int32 [32, 32, 16], P('dom'), may hold values from 0 to 4095, as said below
- send_count: int32 [32, 32], P('dom'), may hold values from 0 to 16, as said below
- cotangent: bfloat16 [131072, 256], P('dom'), may hold values from -6 to 6
Outputs:
- activation: bfloat16 [131072, 256], P('dom')
- grad_features: bfloat16 [131072, 256], P('dom')
- grad_weight: float32 [256, 256], replicated
- grad_bias: float32 [256], replicated
Inputs may be any that keep to these rules, and one draw needn't show every extreme that they name: `tile_count`: each partition uses at least a quarter of its slots; in every draw two partitions use all 256. `send_rows`: for each sender and reader the 16 listed rows are distinct. `send_count`: in every draw one reader receives 16 rows from every partition.
All inputs are finite; a program needn't handle non-finite values.
Results may differ from a plain program's by a relative error of at most 0.0061.
Values may be sent and summed in bfloat16 or wider, within the bound.
A program may use at most 192 MiB of HBM per device.

v0:
```python
import math

import jax
import jax.numpy as jnp
from jax import lax
from jax.sharding import PartitionSpec as P


def deposit(runnings, tile_set, sources, chosen, sink_parts, inside, pattern):
    fetched = sources[chosen]
    products = jnp.einsum(pattern, tile_set, fetched, preferred_element_type=jnp.float32)
    results = []
    for running, (targets, wanted) in zip(runnings, sink_parts):
        masked = jnp.where((inside & wanted)[:, None, None], products, 0.0)
        results.append(running.at[targets].add(masked))
    return tuple(results)


def tile_pass(tile_set, sources, chosen, sinks, tile_total, pattern):
    number = tile_set.shape[0]
    tile_edge = tile_set.shape[1]
    width = sources.shape[2]
    initial = tuple(
        (
            jnp.zeros((target_count, tile_edge, width), jnp.float32)
            for targets, target_count, wanted in sinks
        )
    )
    portion = math.gcd(number, 32)
    passes = (tile_total + portion - 1) // portion

    def advance(turn_index, runnings):
        offset = turn_index * portion
        part_tiles = lax.dynamic_slice_in_dim(tile_set, offset, portion, 0)
        part_chosen = lax.dynamic_slice_in_dim(chosen, offset, portion, 0)
        sink_parts = [
            (
                lax.dynamic_slice_in_dim(targets, offset, portion, 0),
                lax.dynamic_slice_in_dim(wanted, offset, portion, 0),
            )
            for targets, target_count, wanted in sinks
        ]
        inside = offset + lax.iota(jnp.int32, portion) < tile_total
        return deposit(runnings, part_tiles, sources, part_chosen, sink_parts, inside, pattern)

    return lax.fori_loop(0, passes, advance, initial)


def body(
    features,
    weight,
    bias_vector,
    tile_values,
    tile_row,
    tile_col,
    tile_count,
    send_rows,
    send_count,
    cotangent,
):
    local_rows, feature_width = features.shape
    devices = lax.axis_size("dom")
    slot_count = send_rows.shape[2]
    tile_edge = tile_values.shape[1]
    own_blocks = local_rows // tile_edge
    halo_blocks = devices * slot_count // tile_edge
    ext_count = own_blocks + halo_blocks
    tile_total = tile_count[0]
    column_ids = tile_col[0]
    row_ids = tile_row[0]
    everywhere = jnp.ones(column_ids.shape, jnp.bool_)
    slot_index = lax.broadcasted_iota(jnp.int32, (devices, slot_count), 1)
    live_slots = slot_index < send_count[0][:, None]
    picked = features[send_rows[0]]
    outgoing = jnp.where(live_slots[:, :, None], picked, jnp.zeros_like(picked))
    halo_rows = lax.all_to_all(outgoing, "dom", split_axis=0, concat_axis=0, tiled=True)
    halo_flat = halo_rows.reshape(devices * slot_count, feature_width)
    extended = jnp.concatenate([features, halo_flat], 0)
    ext_blocks = extended.reshape(ext_count, tile_edge, feature_width)
    (aggregated,) = tile_pass(
        tile_values,
        ext_blocks,
        column_ids,
        [(row_ids, own_blocks, everywhere)],
        tile_total,
        "kij,kjf->kif",
    )
    aggregated = aggregated.reshape(local_rows, feature_width).astype(jnp.bfloat16)
    linear = jnp.dot(aggregated, weight, preferred_element_type=jnp.float32) + bias_vector
    sigmoid_value = jax.nn.sigmoid(linear)
    activation = (linear * sigmoid_value).astype(jnp.bfloat16)
    slope_value = sigmoid_value * (1.0 + linear * (1.0 - sigmoid_value))
    grad_linear = (cotangent.astype(jnp.float32) * slope_value).astype(jnp.bfloat16)
    weight_part = jnp.dot(aggregated.T, grad_linear, preferred_element_type=jnp.float32)
    bias_part = jnp.sum(grad_linear.astype(jnp.float32), axis=0)
    grad_mixed = jnp.dot(grad_linear, weight.T, preferred_element_type=jnp.float32).astype(
        jnp.bfloat16
    )
    mixed_blocks = grad_mixed.reshape(own_blocks, tile_edge, feature_width)
    (spread_back,) = tile_pass(
        tile_values,
        mixed_blocks,
        row_ids,
        [(column_ids, ext_count, everywhere)],
        tile_total,
        "kji,kjf->kif",
    )
    spread_back = spread_back.reshape(ext_count * tile_edge, feature_width)
    own_grad = spread_back[:local_rows]
    halo_grad = (
        spread_back[local_rows:].astype(jnp.bfloat16).reshape(devices, slot_count, feature_width)
    )
    returned = lax.all_to_all(halo_grad, "dom", split_axis=0, concat_axis=0, tiled=True).astype(
        jnp.float32
    )
    returned = jnp.where(live_slots[:, :, None], returned, jnp.zeros_like(returned))
    collected = (
        jnp.zeros((local_rows, feature_width), jnp.float32)
        .at[send_rows[0].reshape(-1)]
        .add(returned.reshape(-1, feature_width))
    )
    grad_features = (own_grad + collected).astype(jnp.bfloat16)
    weight_sum, bias_sum = lax.psum((weight_part, bias_part), "dom")
    norm_scale = float(local_rows * devices) ** (-0.5)
    return (activation, grad_features, weight_sum * norm_scale, bias_sum * norm_scale)


def solution(mesh):
    return jax.shard_map(
        body,
        mesh=mesh,
        in_specs=(
            P("dom", None),
            P(),
            P(),
            P("dom", None, None),
            P("dom", None),
            P("dom", None),
            P("dom"),
            P("dom", None, None),
            P("dom", None),
            P("dom", None),
        ),
        out_specs=(P("dom", None), P("dom", None), P(), P()),
        check_vma=False,
    )
```

profile of v0, /device:TPU:0, one launch (start us, length us, event | category | flops | bytes accessed | tf_op | source)
XLA Modules:
  0.0 477.1 jit_solution(924079712619475625)
XLA Ops:
  8.9 3.4 gather_fusion.2
  13.2 7.3 %all-to-all-start = ((bf16[32,16,256]{2,1,0:T(8,128)(2,1)}), bf16[32,16,256]{2,1,0:T(8,128)(2,1)S(1)}, u32[]{:S(2)}, u32[]{:S(2)}) async-start(bf16[32,16,256]{2,1,0:T(8,128)(2,1)} %broadcast_select_fusion), calls=%async_computation | async-start | bytes 524288 | tf_op jit(solution)/shard_map/all_to_all | solution.py:76
  22.1 9.1 %all-to-all-done = bf16[32,16,256]{2,1,0:T(8,128)(2,1)S(1)} async-done(((bf16[32,16,256]{2,1,0:T(8,128)(2,1)}), bf16[32,16,256]{2,1,0:T(8,128)(2,1)S(1)}, u32[]{:S(2)}, u32[]{:S(2)}) %all-to-all-start) | async-done | bytes 262176 | tf_op jit(solution)/shard_map/all_to_all | solution.py:76
  32.8 2.5 broadcast_in_dim.66
  35.2 50.7 %while.20 = (s32[]{:T(128)}, f32[32,128,256]{2,1,0:T(8,128)}, s32[]{:T(128)}, s32[256]{0:T(256)S(1)}, s32[]{:T(128)}, /*index=5*/bf16[256,128,128]{2,1,0:T(8,128...) while((s32[]{:T(128)}, f32[32,128,256]{2,1,0:T(8,128)}, ...), condition=%wide.region_2.3_spmd, body=%wide.region_0.2_spmd.sunk | while | flops 270533888 | bytes 24122484 | solution.py:46
  36.0 2.3 gather_fusion
  38.3 3.9 convolution_select_fusion.4
  42.2 10.0 %scatter_fusion = f32[32,128,256]{2,1,0:T(8,128)} fusion(f32[32,128,256]{2,1,0:T(8,128)} %get-tuple-element.268, s32[32]{0:T(128)S(1)} %get-tuple-element.243, f32[32,128,256]{2,1,0:T(8,128)} %convolution_select_fusion.4), kind=kCustom, calls=%fused_computation.3.clone.1 | custom fusion | flops 1048576 | bytes 12583040 | tf_op jit(solution)/shard_map/while/body/scatter-add | solution.py:15
  52.9 2.3 gather_fusion
  55.3 3.9 convolution_select_fusion.4
  59.1 10.0 %scatter_fusion = f32[32,128,256]{2,1,0:T(8,128)} fusion(f32[32,128,256]{2,1,0:T(8,128)} %get-tuple-element.268, s32[32]{0:T(128)S(1)} %get-tuple-element.243, f32[32,128,256]{2,1,0:T(8,128)} %convolution_select_fusion.4), kind=kCustom, calls=%fused_computation.3.clone.1 | custom fusion | flops 1048576 | bytes 12583040 | tf_op jit(solution)/shard_map/while/body/scatter-add | solution.py:15
  69.9 2.3 gather_fusion
  72.2 3.9 convolution_select_fusion.4
  76.1 9.9 %scatter_fusion = f32[32,128,256]{2,1,0:T(8,128)} fusion(f32[32,128,256]{2,1,0:T(8,128)} %get-tuple-element.268, s32[32]{0:T(128)S(1)} %get-tuple-element.243, f32[32,128,256]{2,1,0:T(8,128)} %convolution_select_fusion.4), kind=kCustom, calls=%fused_computation.3.clone.1 | custom fusion | flops 1048576 | bytes 12583040 | tf_op jit(solution)/shard_map/while/body/scatter-add | solution.py:15
  85.9 2.6 convert_element_type.32
  88.8 3.3 convert_reduce_fusion
  94.2 2.7 broadcast_in_dim.69
  96.9 51.0 %while.21 = (s32[]{:T(128)}, f32[36,128,256]{2,1,0:T(8,128)}, s32[]{:T(128)}, s32[256]{0:T(256)S(1)}, s32[]{:T(128)}, /*index=5*/bf16[256,128,128]{2,1,0:T(8,128...) while((s32[]{:T(128)}, f32[36,128,256]{2,1,0:T(8,128)}, ...), condition=%wide.region_5.6_spmd, body=%wide.region_3.5_spmd.sunk | while | flops 270533888 | bytes 24122484 | solution.py:46
  97.6 2.3 gather_fusion.1
  99.9 4.1 convolution_select_fusion.5
  104.0 9.9 %scatter_fusion.1 = f32[36,128,256]{2,1,0:T(8,128)} fusion(f32[36,128,256]{2,1,0:T(8,128)} %get-tuple-element.304, s32[32]{0:T(128)S(1)} %get-tuple-element.253, f32[32,128,256]{2,1,0:T(8,128)} %convolution_select_fusion.5), kind=kCustom, calls=%fused_computation.4.clone.1 | custom fusion | flops 1048576 | bytes 12583040 | tf_op jit(solution)/shard_map/while/body/scatter-add | solution.py:15
  116.9 4.1 convolution_select_fusion.5
  121.0 9.9 %scatter_fusion.1 = f32[36,128,256]{2,1,0:T(8,128)} fusion(f32[36,128,256]{2,1,0:T(8,128)} %get-tuple-element.304, s32[32]{0:T(128)S(1)} %get-tuple-element.253, f32[32,128,256]{2,1,0:T(8,128)} %convolution_select_fusion.5), kind=kCustom, calls=%fused_computation.4.clone.1 | custom fusion | flops 1048576 | bytes 12583040 | tf_op jit(solution)/shard_map/while/body/scatter-add | solution.py:15
  133.9 4.1 convolution_select_fusion.5
  138.0 9.9 %scatter_fusion.1 = f32[36,128,256]{2,1,0:T(8,128)} fusion(f32[36,128,256]{2,1,0:T(8,128)} %get-tuple-element.304, s32[32]{0:T(128)S(1)} %get-tuple-element.253, f32[32,128,256]{2,1,0:T(8,128)} %convolution_select_fusion.5), kind=kCustom, calls=%fused_computation.4.clone.1 | custom fusion | flops 1048576 | bytes 12583040 | tf_op jit(solution)/shard_map/while/body/scatter-add | solution.py:15
  149.6 171.4 %all-to-all-start.1 = ((bf16[32,16,256]{2,1,0:T(8,128)(2,1)}), bf16[32,16,256]{2,1,0:T(8,128)(2,1)S(1)}, u32[]{:S(2)}, u32[]{:S(2)}) async-start(bf16[32,16,256]{2,1,0:T(8,128)(2,1)} %bitcast.12), calls=%async_computation.1 | async-start | bytes 524288 | tf_op jit(solution)/shard_map/all_to_all | solution.py:113
  321.0 3.7 fusion.4
  324.7 4.7 slice.11
  329.4 40.7 %psum.15 = f32[256]{0:T(256)S(1)} all-reduce(f32[256]{0:T(256)S(1)} %get-tuple-element.140), channel_id=1, replica_groups=mesh['dom'=32] {'dom'}, use_global_device_ids=true, to_apply=%region_9.10 | all-reduce | flops 256 | bytes 2048 | tf_op jit(solution)/shard_map/psum | solution.py:123
  370.6 86.9 %all-reduce.2.cloned.1.call-done = f32[256,256]{1,0:T(8,128)} async-done(((f32[256,256]{1,0:T(8,128)}), f32[256,256]{1,0:T(8,128)}) %all-reduce.2.cloned.1.call-update) | async-done | bytes 262160 | tf_op jit(solution)/shard_map/psum | solution.py:123
  459.3 7.2 %scatter_fusion.2 = f32[4096,256]{1,0:T(8,128)} fusion(f32[4096,256]{1,0:T(8,128)} %bitcast.32, s32[512]{0:T(512)S(1)} %bitcast.40, f32[512,256]{1,0:T(8,128)S(1)} %bitcast.35), kind=kCustom, calls=%fused_computation.5 | custom fusion | flops 131072 | bytes 1574912 | tf_op jit(solution)/shard_map/scatter-add | solution.py:120
  466.5 3.7 convert_element_type.40
  (54 shorter events, 20.6 us)
Async XLA Ops:
  7.2 81.4 %copy-start = (bf16[256,256]{1,0:T(8,128)(2,1)S(1)}, bf16[256,256]{1,0:T(8,128)(2,1)}, u32[]{:S(2)}) copy-start(bf16[256,256]{1,0:T(8,128)(2,1)} %param.15) | copy-start | bytes 393220
  7.2 23.9 %copy-start.1 = (bf16[4096,256]{1,0:T(8,128)(2,1)S(1)}, bf16[4096,256]{1,0:T(8,128)(2,1)}, u32[]{:S(2)}) copy-start(bf16[4096,256]{1,0:T(8,128)(2,1)} %param.14) | copy-start | bytes 6291460
  13.2 17.9 %all-to-all-start = ((bf16[32,16,256]{2,1,0:T(8,128)(2,1)}), bf16[32,16,256]{2,1,0:T(8,128)(2,1)S(1)}, u32[]{:S(2)}, u32[]{:S(2)}) async-start(bf16[32,16,256]{2,1,0:T(8,128)(2,1)} %broadcast_select_fusion), calls=%async_computation | async-start | bytes 524288 | tf_op jit(solution)/shard_map/all_to_all | solution.py:76
  31.1 4.1 copy-start.4
  31.1 4.1 copy-start.5
  85.9 2.9 copy-start.6
  85.9 2.9 copy-start.7
  88.6 3.6 copy-start.3
  92.1 4.7 copy-start.2
  149.6 309.6 %all-to-all-start.1 = ((bf16[32,16,256]{2,1,0:T(8,128)(2,1)}), bf16[32,16,256]{2,1,0:T(8,128)(2,1)S(1)}, u32[]{:S(2)}, u32[]{:S(2)}) async-start(bf16[32,16,256]{2,1,0:T(8,128)(2,1)} %bitcast.12), calls=%async_computation.1 | async-start | bytes 524288 | tf_op jit(solution)/shard_map/all_to_all | solution.py:113
  321.0 136.5 %all-reduce.2.cloned.1.call-start = ((), (), s32[]{:S(2)}) async-start(), calls=%async_computation.2 | async-start | bytes 524288 | tf_op jit(solution)/shard_map/psum | solution.py:123
Sparse Core Ops, SparseCore 0:
  329.5 127.9 all-reduce.1
where the time goes:
time: 479 us; the launch traced here: 477 us
  starting transfers between devices  179 us (37%)
  waiting for transfers between devices  96 us (20%)
  other arithmetic  83.9 us (18%)
  blocking collectives  40.7 us (8%)
  matrix products  32.9 us (7%)
  local copies, waits for them, and re-layouts  30.1 us (6%)
  between operations  14.8 us (3%)
    all_to_all x1, starting transfers between devices, body(): lax.all_to_all(halo_grad, 'dom', split_axis=0, concat_axis=0, tiled=True)  171 us
    psum x1, waiting for transfers between devices, body(): weight_sum, bias_sum = lax.psum((weight_part, bias_part), 'dom')  86.9 us
    scatter-add x6, other arithmetic, deposit(): results.append(running.at[targets].add(masked))  59.4 us
    psum x1, blocking collectives, body(): weight_sum, bias_sum = lax.psum((weight_part, bias_part), 'dom')  40.7 us
    dot_general x6, matrix products, deposit(): jnp.einsum(pattern, tile_set, fetched, preferred_element_type=jnp.float32)  23.8 us
    gather x6, local copies, waits for them, and re-layouts, deposit(): fetched = sources[chosen]  13.9 us
  transfers between devices with their start and end apart: 3, of which 2 were waited for; matrix products, arithmetic and copies ran while one was open for 2% of the time, Pallas kernels for 0%

commit v1 on v0

v1 whole, which is shorter than its diff:
```python
import functools
import math

import jax
import jax.numpy as jnp
from jax import lax
from jax.experimental import pallas as pl
from jax.experimental.pallas import tpu as pltpu
from jax.sharding import PartitionSpec as P

MESH = pl.DeviceIdType.MESH
VMEM = pltpu.VMEM
f32 = jnp.float32
bf16 = jnp.bfloat16


def greet(n, me):
    barrier = pltpu.get_barrier_semaphore()

    def signal(i, carry):
        pl.semaphore_signal(
            barrier, inc=1, device_id=(lax.rem(me + i, n),), device_id_type=MESH
        )
        return carry

    lax.fori_loop(1, n, signal, 0)
    return barrier


def push(n, me, src, dst, send_sem, recv_sem, i):
    peer = lax.rem(me + i, n)
    return pltpu.make_async_remote_copy(
        src_ref=src(peer),
        dst_ref=dst.at[me],
        send_sem=send_sem.at[i],
        recv_sem=recv_sem.at[i],
        device_id=(peer,),
        device_id_type=MESH,
    )


def gather_kernel(n, chosen_ref, features_ref, halo_ref, total, sent, landed, send_sem, recv_sem):
    me = lax.axis_index("dom")
    barrier = greet(n, me)
    slots = chosen_ref.shape[0]
    rows = features_ref.shape[0]
    step = math.gcd(rows, 512)
    for c in range(rows // step):
        ids = lax.broadcasted_iota(jnp.int32, (slots, step), 1) + c * step
        hot = jnp.where(ids == chosen_ref[...], 1.0, 0.0).astype(bf16)
        part = jnp.dot(hot, features_ref[pl.ds(c * step, step), :], preferred_element_type=f32)
        if c == 0:
            total[...] = part
        else:
            total[...] += part
    sent[...] = total[...].astype(bf16).reshape(sent.shape)
    pl.semaphore_wait(barrier, n - 1)
    copy = functools.partial(push, n, me, lambda p: sent.at[p], landed, send_sem, recv_sem)

    def start(i, carry):
        copy(i).start()
        return carry

    def finish(i, carry):
        copy(i).wait()
        return carry

    lax.fori_loop(1, n, start, 0)
    landed[me] = sent[me]
    lax.fori_loop(1, n, finish, 0)
    halo_ref[...] = landed[...]


def exchange_gather(n, chosen, features, slot_count):
    width = features.shape[1]
    slots = chosen.shape[0]
    block = (n, slot_count, width)
    return pl.pallas_call(
        functools.partial(gather_kernel, n),
        out_shape=jax.ShapeDtypeStruct(block, bf16),
        in_specs=[pl.BlockSpec(memory_space=VMEM)] * 2,
        out_specs=pl.BlockSpec(memory_space=VMEM),
        scratch_shapes=[
            VMEM((slots, width), f32),
            VMEM(block, bf16),
            VMEM(block, bf16),
            pltpu.SemaphoreType.DMA((n,)),
            pltpu.SemaphoreType.DMA((n,)),
        ],
        compiler_params=pltpu.CompilerParams(collective_id=0, has_side_effects=True),
        name="gather_exchange",
    )(chosen, features)


GROUP = 8
CHUNK = 16


def local_kernel(
    tile_row, tile_col, tile_count, features, halo, tiles, cotangent, weight, bias,
    activation, own_grad, halo_grad, weight_part, bias_part,
    source, held, cot, act, mixed, forward, backward, spread, wsum, bsum,
    in_sem, tile_sem, cot_sem, act_sem, out_sem,
):
    own = features.shape[0]
    ext = own + halo.shape[0]
    number = tiles.shape[0]
    chunk = math.gcd(number, CHUNK)
    group = math.gcd(chunk, GROUP)
    total = tile_count[0]
    chunks = (total + chunk - 1) // chunk

    def tile_copy(c):
        span = pl.ds(c * chunk, chunk)
        return pltpu.make_async_copy(tiles.at[span], held.at[span], tile_sem.at[c])

    copies = [
        pltpu.make_async_copy(features, source.at[pl.ds(0, own)], in_sem.at[0]),
        pltpu.make_async_copy(halo, source.at[pl.ds(own, ext - own)], in_sem.at[1]),
    ]
    for copy in copies:
        copy.start()

    @pl.loop(0, chunks)
    def _(c):
        tile_copy(c).start()

    cot_copy = pltpu.make_async_copy(cotangent, cot, cot_sem)
    cot_copy.start()

    @pl.loop(0, own)
    def _(r):
        forward[r] = jnp.zeros(forward.shape[1:], f32)
        backward[r] = jnp.zeros(backward.shape[1:], f32)

    for r in range(own, ext):
        backward[r] = jnp.zeros(backward.shape[1:], f32)
    for copy in copies:
        copy.wait()

    @pl.loop(0, chunks)
    def _(c):
        tile_copy(c).wait()
        for g in range(chunk // group):
            base = c * chunk + g * group
            for j in range(group):
                k = base + j
                product = jnp.dot(held[k], source[tile_col[0, k]], preferred_element_type=f32)
                target = jnp.where(k < total, tile_row[0, k], own)
                forward[target] += product

    cot_copy.wait()
    edge = tiles.shape[1]
    step = math.gcd(own, 4)
    width = weight.shape[0]
    wsum[...] = jnp.zeros_like(wsum)
    bsum[...] = jnp.zeros_like(bsum)

    def act_copy(b):
        span = pl.ds(b * step, step)
        return pltpu.make_async_copy(act.at[span], activation.at[span], act_sem.at[b])

    @pl.loop(0, own // step)
    def _(b):
        span = pl.ds(b * step, step)
        agg = forward[span].astype(bf16).reshape(step * edge, width)
        linear = jnp.dot(agg, weight[...], preferred_element_type=f32) + bias[...]
        sig = jax.nn.sigmoid(linear)
        act[span] = (linear * sig).astype(bf16).reshape(step, edge, width)
        act_copy(b).start()
        slope = sig * (1.0 + linear * (1.0 - sig))
        grad = (cot[span].reshape(step * edge, width).astype(f32) * slope).astype(bf16)
        wsum[...] += lax.dot_general(
            agg, grad, (((0,), (0,)), ((), ())), preferred_element_type=f32
        )
        bsum[...] += jnp.sum(grad.astype(f32), axis=0, keepdims=True)
        back = lax.dot_general(
            grad, weight[...], (((1,), (1,)), ((), ())), preferred_element_type=f32
        )
        mixed[span] = back.astype(bf16).reshape(step, edge, width)

    @pl.loop(0, chunks * (chunk // group))
    def _(g):
        for j in range(group):
            k = g * group + j
            product = lax.dot_general(
                held[k], mixed[tile_row[0, k]], (((0,), (0,)), ((), ())),
                preferred_element_type=f32,
            )
            target = jnp.where(k < total, tile_col[0, k], ext)
            backward[target] += product

    def out_copy(b):
        span = pl.ds(b * step, step)
        return pltpu.make_async_copy(spread.at[span], own_grad.at[span], out_sem.at[b])

    @pl.loop(0, own // step)
    def _(b):
        span = pl.ds(b * step, step)
        spread[span] = backward[span].astype(bf16)
        out_copy(b).start()

    halo_grad[...] = backward[pl.ds(own, ext - own)].astype(bf16)
    pieces, piece_rows = weight_part.shape[:2]
    for p in range(pieces):
        weight_part[p] = wsum[pl.ds(p * piece_rows, piece_rows), :].astype(bf16)
    bias_part[...] = bsum[...]

    @pl.loop(0, own // step)
    def _(b):
        act_copy(b).wait()
        out_copy(b).wait()


def local_pass(n, tile_row, tile_col, tile_count, features, halo, tiles, cotangent, weight, bias):
    own, edge, width = features.shape
    ext = own + halo.shape[0]
    number = tiles.shape[0]
    chunk = math.gcd(number, CHUNK)
    steps = own // math.gcd(own, 4)
    anywhere = pl.BlockSpec(memory_space=pltpu.HBM)
    smem = pl.BlockSpec(memory_space=pltpu.SMEM)
    vmem = pl.BlockSpec(memory_space=VMEM)
    dma = pltpu.SemaphoreType.DMA
    return pl.pallas_call(
        local_kernel,
        out_shape=(
            jax.ShapeDtypeStruct(features.shape, bf16),
            jax.ShapeDtypeStruct(features.shape, bf16),
            jax.ShapeDtypeStruct(halo.shape, bf16),
            jax.ShapeDtypeStruct((n, width // n, width), bf16),
            jax.ShapeDtypeStruct((1, width), f32),
        ),
        in_specs=[smem] * 3 + [anywhere] * 4 + [vmem] * 2,
        out_specs=(anywhere, anywhere, vmem, vmem, vmem),
        scratch_shapes=[
            VMEM((ext, edge, width), bf16),
            VMEM(tiles.shape, bf16),
            VMEM(features.shape, bf16),
            VMEM(features.shape, bf16),
            VMEM(features.shape, bf16),
            VMEM((own + 1, edge, width), f32),
            VMEM((ext + 1, edge, width), f32),
            VMEM(features.shape, bf16),
            VMEM((width, width), f32),
            VMEM((1, width), f32),
            dma((2,)),
            dma((number // chunk,)),
            dma,
            dma((steps,)),
            dma((steps,)),
        ],
        compiler_params=pltpu.CompilerParams(vmem_limit_bytes=56 * 1024 * 1024),
        name="local_pass",
    )(tile_row, tile_col, tile_count, features, halo, tiles, cotangent, weight, bias)


def return_kernel(
    n, scale, halo_ref, weight_ref, bias_ref, returned_ref, wsum_ref, bsum_ref,
    halo_in, weight_in, bias_in, piece, pieces_in,
    halo_s, halo_r, weight_s, weight_r, bias_s, bias_r, piece_s, piece_r,
):
    me = lax.axis_index("dom")
    barrier = greet(n, me)
    pl.semaphore_wait(barrier, n - 1)
    halo_copy = functools.partial(push, n, me, lambda p: halo_ref.at[p], halo_in, halo_s, halo_r)
    weight_copy = functools.partial(
        push, n, me, lambda p: weight_ref.at[p], weight_in, weight_s, weight_r
    )
    bias_copy = functools.partial(push, n, me, lambda p: bias_ref, bias_in, bias_s, bias_r)
    piece_copy = functools.partial(push, n, me, lambda p: piece, pieces_in, piece_s, piece_r)

    def over(step):
        def turn(i, carry):
            step(i)
            return carry

        lax.fori_loop(1, n, turn, 0)

    def first(i):
        weight_copy(i).start()
        bias_copy(i).start()

    over(first)
    over(lambda i: halo_copy(i).start())
    weight_in[me] = weight_ref[me]
    bias_in[me] = bias_ref[...]
    halo_in[me] = halo_ref[me]
    over(lambda i: weight_copy(i).wait())
    piece[...] = (jnp.sum(weight_in[...].astype(f32), axis=0) * scale).astype(bf16)
    over(lambda i: piece_copy(i).start())
    pieces_in[me] = piece[...]
    over(lambda i: bias_copy(i).wait())
    bsum_ref[...] = jnp.sum(bias_in[...], axis=0) * scale
    over(lambda i: halo_copy(i).wait())
    returned_ref[...] = halo_in[...]
    over(lambda i: piece_copy(i).wait())
    rows = piece.shape[0]
    for p in range(n):
        wsum_ref[pl.ds(p * rows, rows), :] = pieces_in[p].astype(f32)


def exchange_return(n, scale, halo_grad, weight_part, bias_part):
    width = bias_part.shape[1]
    vmem = pl.BlockSpec(memory_space=VMEM)
    return pl.pallas_call(
        functools.partial(return_kernel, n, scale),
        out_shape=(
            jax.ShapeDtypeStruct(halo_grad.shape, bf16),
            jax.ShapeDtypeStruct((width, width), f32),
            jax.ShapeDtypeStruct((1, width), f32),
        ),
        in_specs=[vmem] * 3,
        out_specs=(vmem,) * 3,
        scratch_shapes=[
            VMEM(halo_grad.shape, bf16),
            VMEM(weight_part.shape, bf16),
            VMEM((n,) + bias_part.shape, f32),
            VMEM(weight_part.shape[1:], bf16),
            VMEM(weight_part.shape, bf16),
        ]
        + [pltpu.SemaphoreType.DMA((n,))] * 8,
        compiler_params=pltpu.CompilerParams(collective_id=1, has_side_effects=True),
        name="return_exchange",
    )(halo_grad, weight_part, bias_part)


def scatter_kernel(chosen, returned, own_grad, out):
    rows = out.shape[0]
    base = pl.program_id(0) * rows
    ids = lax.broadcasted_iota(jnp.int32, (rows, chosen.shape[1]), 0) + base
    hot = jnp.where(ids == chosen[...], 1.0, 0.0).astype(bf16)
    collected = jnp.dot(hot, returned[...], preferred_element_type=f32)
    out[...] = (own_grad[...].astype(f32) + collected).astype(bf16)


def scatter_add(chosen, returned, own_grad):
    rows, width = own_grad.shape
    step = math.gcd(rows, 1024)
    whole = lambda i: (0, 0)
    return pl.pallas_call(
        scatter_kernel,
        out_shape=jax.ShapeDtypeStruct(own_grad.shape, bf16),
        grid=(rows // step,),
        in_specs=[
            pl.BlockSpec(chosen.shape, whole),
            pl.BlockSpec(returned.shape, whole),
            pl.BlockSpec((step, width), lambda i: (i, 0)),
        ],
        out_specs=pl.BlockSpec((step, width), lambda i: (i, 0)),
        name="scatter_add",
    )(chosen, returned, own_grad)


def body(
    features, weight, bias_vector, tile_values, tile_row, tile_col, tile_count, send_rows,
    send_count, cotangent,
):
    rows, width = features.shape
    n = lax.axis_size("dom")
    slot_count = send_rows.shape[2]
    edge = tile_values.shape[1]
    own = rows // edge
    slots = n * slot_count
    slot_index = lax.broadcasted_iota(jnp.int32, (n, slot_count), 1)
    chosen = jnp.where(slot_index < send_count[0][:, None], send_rows[0], -1)
    halo = exchange_gather(n, chosen.reshape(slots, 1), features, slot_count)
    blocks = lambda a: a.reshape(-1, edge, width)
    activation, own_grad, halo_grad, weight_part, bias_part = local_pass(
        n, tile_row, tile_col, tile_count, blocks(features), blocks(halo), tile_values,
        blocks(cotangent), weight, bias_vector.reshape(1, width),
    )
    scale = float(rows * n) ** (-0.5)
    returned, weight_sum, bias_sum = exchange_return(
        n, scale, halo_grad.reshape(n, slot_count, width), weight_part, bias_part
    )
    grad_features = scatter_add(
        chosen.reshape(1, slots), returned.reshape(slots, width), own_grad.reshape(rows, width)
    )
    return (activation.reshape(rows, width), grad_features, weight_sum, bias_sum.reshape(width))


def solution(mesh):
    return jax.shard_map(
        body,
        mesh=mesh,
        in_specs=(
            P("dom", None),
            P(),
            P(),
            P("dom", None, None),
            P("dom", None),
            P("dom", None),
            P("dom"),
            P("dom", None, None),
            P("dom", None),
            P("dom", None),
        ),
        out_specs=(P("dom", None), P("dom", None), P(), P()),
        check_vma=False,
    )
```

time: 479 us -> 75.9 us (0.16)
  starting transfers between devices: 179 us -> 0 us
  waiting for transfers between devices: 96 us -> 0 us
  other arithmetic: 83.9 us -> 2.06 us
  Pallas kernels: 0 us -> 69.1 us
  blocking collectives: 40.7 us -> 0 us
  matrix products: 32.9 us -> 0 us
  local copies, waits for them, and re-layouts: 30.1 us -> 2.56 us
  between operations: 14.8 us -> 1.34 us
    all_to_all x2 -> x0, starting transfers between devices: 179 us -> none  [the longest x1 171 us: body(): lax.all_to_all(halo_grad, 'dom', split_axis=0, concat_axis=0, tiled=True)]
    psum x1 -> x0, waiting for transfers between devices: 86.9 us -> none  [body(): weight_sum, bias_sum = lax.psum((weight_part, bias_part), 'dom')]
    pallas_call x0 -> x4, Pallas kernels: none -> 69.1 us  [the longest x1 33.2 us: exchange_return(): pl.pallas_call(functools.partial(return_kernel, n, scale), out_shape=(jax...]
    scatter-add x7 -> x0, other arithmetic: 66.7 us -> none  [the longest x6 59.4 us: deposit(): results.append(running.at[targets].add(masked))]
    psum x1 -> x0, blocking collectives: 40.7 us -> none  [body(): weight_sum, bias_sum = lax.psum((weight_part, bias_part), 'dom')]
    dot_general x9 -> x0, matrix products: 32.9 us -> none  [the longest x6 23.8 us: deposit(): jnp.einsum(pattern, tile_set, fetched, preferred_element_type=jnp.float32)]
    gather x7 -> x0, local copies, waits for them, and re-layouts: 17.3 us -> none  [the longest x6 13.9 us: deposit(): fetched = sources[chosen]]
    all_to_all x2 -> x0, waiting for transfers between devices: 9.06 us -> none  [the longest x1 9.06 us: body(): lax.all_to_all(outgoing, 'dom', split_axis=0, concat_axis=0, tiled=True)]
  transfers between devices with their start and end apart: 3 -> 0, of which waited for: 2 -> 0; matrix products, arithmetic and copies ran while one was open for 2% -> 0% of each run, Pallas kernels for 0% -> 0%
where the time goes in v1:
time: 75.9 us; the launch traced here: 75 us
  Pallas kernels  69.1 us (91%)
  local copies, waits for them, and re-layouts  2.56 us (3%)
  other arithmetic  2.06 us (3%)
  between operations  1.34 us (2%)
    pallas_call x1, Pallas kernels, exchange_return(): pl.pallas_call(functools.partial(return_kernel, n, scale), out_shape=(jax...  33.2 us
    pallas_call x1, Pallas kernels, local_pass(): pl.pallas_call(local_kernel, out_shape=(jax.ShapeDtypeStruct(features.sha...  16.5 us
    pallas_call x1, Pallas kernels, exchange_gather(): pl.pallas_call(functools.partial(gather_kernel, n), out_shape=jax.ShapeDt...  14.7 us
    pallas_call x1, Pallas kernels, scatter_add(): pl.pallas_call(scatter_kernel, out_shape=jax.ShapeDtypeStruct(own_grad.sh...  4.7 us
    unnamed x7, local copies, waits for them, and re-layouts  2.05 us

profile of v1, /device:TPU:0, one launch (start us, length us, event | category | flops | bytes accessed | tf_op | source)
XLA Modules:
  0.0 75.0 jit_solution(6068745473585300940)
XLA Ops:
  1.3 0.7 iota_compare_fusion
  2.0 0.1 lt.34
  2.1 0.8 %copy.16 = s32[1,32,16]{2,1,0:T(8,128)S(1)} copy(s32[1,32,16]{1,2,0:T(8,128)} %param.17) | data formatting | bytes 4096 | tf_op args[7]
  2.9 0.1 squeeze.6
  3.0 0.6 broadcast_select_fusion.1.chosen
  3.6 0.2 lt.35
  3.7 0.2 squeeze.7
  3.9 0.7 broadcast_select_fusion.chosen_ref
  4.6 14.7 %gather_exchange.1 = bf16[32,16,256]{2,1,0:T(8,128)(2,1)} custom-call(s32[512,1]{1,0:T(8,128)} %broadcast_select_fusion.chosen_ref, bf16[4096,256]{1,0:T(8,128)(2,1)} %features_ref.1), custom_call_target="tpu_custom_call" | custom-call | tf_op jit(solution)/shard_map/gather_exchange/pallas_call | solution.py:78
  19.4 16.5 %local_pass.1 = (bf16[32,128,256]{2,1,0:T(8,128)(2,1)}, bf16[32,128,256]{2,1,0:T(8,128)(2,1)}, bf16[4,128,256]{2,1,0:T(8,128)(2,1)}, bf16[32,8,256]{2,1,0:T(8,128)(2,1)}, f32[1,256]{1,0:T(1,128)}) custom-call(s32[1,256]{1,0:T(1,128)} %tile_row.1, s32[1,256]{1,0:T(1,128)} %tile_col.1, s32[1]{0:T(128)S(6)} %copy.22.tile_count, bf16[32,128,256]{2,1,0:T(8,128)(2,1)} %bitcast.10, ...), custom_call_target="tpu_custom_call" | custom-call | tf_op jit(solution)/shard_map/local_pass/pallas_call | solution.py:225
  35.8 33.2 %return_exchange.1 = (bf16[32,16,256]{2,1,0:T(8,128)(2,1)}, f32[256,256]{1,0:T(8,128)}, f32[1,256]{1,0:T(1,128)}) custom-call(bf16[32,16,256]{2,1,0:T(8,128)(2,1)} %bitcast.15, bf16[32,8,256]{2,1,0:T(8,128)(2,1)} %get-tuple-element.14.weight_ref, f32[1,256]{1,0:T(1,128)} %get-tuple-element.15.bias_ref), custom_call_target="tpu_custom_call" | custom-call | tf_op jit(solution)/shard_map/return_exchange/pallas_call | solution.py:306
  69.0 0.0 copy-start
  69.1 0.0 copy-start.1
  69.1 4.7 %scatter_add.1 = bf16[4096,256]{1,0:T(8,128)(2,1)} custom-call(s32[1,512]{1,0:T(1,128)} %broadcast_select_fusion.1.chosen, bf16[512,256]{1,0:T(8,128)(2,1)} %bitcast.14, bf16[4096,256]{1,0:T(8,128)(2,1)} %bitcast.11), custom_call_target="tpu_custom_call" | custom-call | tf_op jit(solution)/shard_map/scatter_add/pallas_call | solution.py:341
  73.8 0.0 copy-done
  73.8 0.7 copy.23
  74.5 0.0 copy-done.1
  74.5 0.6 copy.24
Async XLA Ops:
  69.0 4.7 %copy-start = (f32[256,256]{1,0:T(8,128)S(1)}, f32[256,256]{1,0:T(8,128)}, u32[]{:S(2)}) copy-start(f32[256,256]{1,0:T(8,128)} %get-tuple-element.26) | copy-start | bytes 786436
  69.1 5.4 %copy-start.1 = (f32[1,256]{1,0:T(1,128)S(1)}, f32[1,256]{1,0:T(1,128)}, u32[]{:S(2)}) copy-start(f32[1,256]{1,0:T(1,128)} %get-tuple-element.19) | copy-start | bytes 3076

commit v2 on v1

--- a/solution.py
+++ b/solution.py
@@ -39,21 +39,40 @@
     )
 
 
-def gather_kernel(n, chosen_ref, features_ref, halo_ref, total, sent, landed, send_sem, recv_sem):
+def live(count_ref, peer, values):
+    slot = lax.broadcasted_iota(jnp.int32, values.shape, 0)
+    return jnp.where(slot < count_ref[0, peer], values, jnp.zeros_like(values))
+
+
+def gather_kernel(
+    n, count_ref, chosen_ref, features_hbm, halo_ref,
+    features_ref, total, sent, landed, send_sem, recv_sem, load_sem,
+):
     me = lax.axis_index("dom")
-    barrier = greet(n, me)
     slots = chosen_ref.shape[0]
     rows = features_ref.shape[0]
     step = math.gcd(rows, 512)
+    loads = []
+    for c in range(rows // step):
+        span = pl.ds(c * step, step)
+        loads.append(
+            pltpu.make_async_copy(features_hbm.at[span], features_ref.at[span], load_sem.at[c])
+        )
+        loads[c].start()
+    barrier = greet(n, me)
     for c in range(rows // step):
         ids = lax.broadcasted_iota(jnp.int32, (slots, step), 1) + c * step
         hot = jnp.where(ids == chosen_ref[...], 1.0, 0.0).astype(bf16)
+        loads[c].wait()
         part = jnp.dot(hot, features_ref[pl.ds(c * step, step), :], preferred_element_type=f32)
         if c == 0:
             total[...] = part
         else:
             total[...] += part
-    sent[...] = total[...].astype(bf16).reshape(sent.shape)
+    slot_count = sent.shape[1]
+    for p in range(n):
+        block = total[pl.ds(p * slot_count, slot_count), :]
+        sent[p] = live(count_ref, p, block).astype(bf16)
     pl.semaphore_wait(barrier, n - 1)
     copy = functools.partial(push, n, me, lambda p: sent.at[p], landed, send_sem, recv_sem)
 
@@ -71,25 +90,38 @@
     halo_ref[...] = landed[...]
 
 
-def exchange_gather(n, chosen, features, slot_count):
+def exchange_gather(n, send_count, chosen, features, slot_count):
     width = features.shape[1]
     slots = chosen.shape[0]
     block = (n, slot_count, width)
     return pl.pallas_call(
         functools.partial(gather_kernel, n),
         out_shape=jax.ShapeDtypeStruct(block, bf16),
-        in_specs=[pl.BlockSpec(memory_space=VMEM)] * 2,
+        in_specs=[
+            pl.BlockSpec(memory_space=pltpu.SMEM),
+            pl.BlockSpec(memory_space=VMEM),
+            pl.BlockSpec(memory_space=pltpu.HBM),
+        ],
         out_specs=pl.BlockSpec(memory_space=VMEM),
         scratch_shapes=[
+            VMEM(features.shape, bf16),
             VMEM((slots, width), f32),
             VMEM(block, bf16),
             VMEM(block, bf16),
             pltpu.SemaphoreType.DMA((n,)),
             pltpu.SemaphoreType.DMA((n,)),
+            pltpu.SemaphoreType.DMA((features.shape[0] // math.gcd(features.shape[0], 512),)),
         ],
-        compiler_params=pltpu.CompilerParams(collective_id=0, has_side_effects=True),
+        compiler_params=pltpu.CompilerParams(
+            collective_id=0, has_side_effects=True, vmem_limit_bytes=60 * 1024 * 1024
+        ),
+        cost_estimate=pl.CostEstimate(
+            flops=2 * slots * features.shape[0] * width,
+            bytes_accessed=16 * features.size,
+            transcendentals=0,
+        ),
         name="gather_exchange",
-    )(chosen, features)
+    )(send_count, chosen, features)
 
 
 GROUP = 8
@@ -256,11 +288,14 @@
 
 
 def return_kernel(
-    n, scale, halo_ref, weight_ref, bias_ref, returned_ref, wsum_ref, bsum_ref,
-    halo_in, weight_in, bias_in, piece, pieces_in,
+    n, scale, count_ref, chosen_ref, halo_ref, weight_ref, bias_ref, own_hbm,
+    out_hbm, wsum_ref, bsum_ref,
+    halo_in, weight_in, bias_in, piece, pieces_in, returned, own, hot, out, load_sem, out_sem,
     halo_s, halo_r, weight_s, weight_r, bias_s, bias_r, piece_s, piece_r,
 ):
     me = lax.axis_index("dom")
+    load = pltpu.make_async_copy(own_hbm, own, load_sem)
+    load.start()
     barrier = greet(n, me)
     pl.semaphore_wait(barrier, n - 1)
     halo_copy = functools.partial(push, n, me, lambda p: halo_ref.at[p], halo_in, halo_s, halo_r)
@@ -286,6 +321,12 @@
     weight_in[me] = weight_ref[me]
     bias_in[me] = bias_ref[...]
     halo_in[me] = halo_ref[me]
+    rows = own.shape[0]
+    slots = chosen_ref.shape[1]
+    step = math.gcd(rows, 512)
+    for c in range(rows // step):
+        ids = lax.broadcasted_iota(jnp.int32, (step, slots), 0) + c * step
+        hot[pl.ds(c * step, step), :] = jnp.where(ids == chosen_ref[...], 1.0, 0.0).astype(bf16)
     over(lambda i: weight_copy(i).wait())
     piece[...] = (jnp.sum(weight_in[...].astype(f32), axis=0) * scale).astype(bf16)
     over(lambda i: piece_copy(i).start())
@@ -293,63 +334,60 @@
     over(lambda i: bias_copy(i).wait())
     bsum_ref[...] = jnp.sum(bias_in[...], axis=0) * scale
     over(lambda i: halo_copy(i).wait())
-    returned_ref[...] = halo_in[...]
+    slot_count = halo_in.shape[1]
+    for p in range(n):
+        returned[pl.ds(p * slot_count, slot_count), :] = live(
+            count_ref, p, halo_in[p].astype(f32)
+        ).astype(bf16)
+    load.wait()
+    outs = []
+    for c in range(rows // step):
+        span = pl.ds(c * step, step)
+        collected = jnp.dot(hot[span, :], returned[...], preferred_element_type=f32)
+        out[span, :] = (own[span, :].astype(f32) + collected).astype(bf16)
+        outs.append(pltpu.make_async_copy(out.at[span], out_hbm.at[span], out_sem.at[c]))
+        outs[c].start()
     over(lambda i: piece_copy(i).wait())
-    rows = piece.shape[0]
+    piece_rows = piece.shape[0]
     for p in range(n):
-        wsum_ref[pl.ds(p * rows, rows), :] = pieces_in[p].astype(f32)
-
-
-def exchange_return(n, scale, halo_grad, weight_part, bias_part):
-    width = bias_part.shape[1]
+        wsum_ref[pl.ds(p * piece_rows, piece_rows), :] = pieces_in[p].astype(f32)
+    for copy in outs:
+        copy.wait()
+
+
+def exchange_return(n, scale, send_count, chosen, halo_grad, weight_part, bias_part, own_grad):
+    rows, width = own_grad.shape
+    slots = chosen.shape[1]
     vmem = pl.BlockSpec(memory_space=VMEM)
+    hbm = pl.BlockSpec(memory_space=pltpu.HBM)
     return pl.pallas_call(
         functools.partial(return_kernel, n, scale),
         out_shape=(
-            jax.ShapeDtypeStruct(halo_grad.shape, bf16),
+            jax.ShapeDtypeStruct(own_grad.shape, bf16),
             jax.ShapeDtypeStruct((width, width), f32),
             jax.ShapeDtypeStruct((1, width), f32),
         ),
-        in_specs=[vmem] * 3,
-        out_specs=(vmem,) * 3,
+        in_specs=[pl.BlockSpec(memory_space=pltpu.SMEM)] + [vmem] * 4 + [hbm],
+        out_specs=(hbm, vmem, vmem),
         scratch_shapes=[
             VMEM(halo_grad.shape, bf16),
             VMEM(weight_part.shape, bf16),
             VMEM((n,) + bias_part.shape, f32),
             VMEM(weight_part.shape[1:], bf16),
             VMEM(weight_part.shape, bf16),
+            VMEM((slots, width), bf16),
+            VMEM(own_grad.shape, bf16),
+            VMEM((rows, slots), bf16),
+            VMEM(own_grad.shape, bf16),
+            pltpu.SemaphoreType.DMA,
+            pltpu.SemaphoreType.DMA((rows // math.gcd(rows, 512),)),
         ]
         + [pltpu.SemaphoreType.DMA((n,))] * 8,
-        compiler_params=pltpu.CompilerParams(collective_id=1, has_side_effects=True),
+        compiler_params=pltpu.CompilerParams(
+            collective_id=1, has_side_effects=True, vmem_limit_bytes=60 * 1024 * 1024
+        ),
         name="return_exchange",
-    )(halo_grad, weight_part, bias_part)
-
-
-def scatter_kernel(chosen, returned, own_grad, out):
-    rows = out.shape[0]
-    base = pl.program_id(0) * rows
-    ids = lax.broadcasted_iota(jnp.int32, (rows, chosen.shape[1]), 0) + base
-    hot = jnp.where(ids == chosen[...], 1.0, 0.0).astype(bf16)
-    collected = jnp.dot(hot, returned[...], preferred_element_type=f32)
-    out[...] = (own_grad[...].astype(f32) + collected).astype(bf16)
-
-
-def scatter_add(chosen, returned, own_grad):
-    rows, width = own_grad.shape
-    step = math.gcd(rows, 1024)
-    whole = lambda i: (0, 0)
-    return pl.pallas_call(
-        scatter_kernel,
-        out_shape=jax.ShapeDtypeStruct(own_grad.shape, bf16),
-        grid=(rows // step,),
-        in_specs=[
-            pl.BlockSpec(chosen.shape, whole),
-            pl.BlockSpec(returned.shape, whole),
-            pl.BlockSpec((step, width), lambda i: (i, 0)),
-        ],
-        out_specs=pl.BlockSpec((step, width), lambda i: (i, 0)),
-        name="scatter_add",
-    )(chosen, returned, own_grad)
+    )(send_count, chosen, halo_grad, weight_part, bias_part, own_grad)
 
 
 def body(
@@ -362,20 +400,17 @@
     edge = tile_values.shape[1]
     own = rows // edge
     slots = n * slot_count
-    slot_index = lax.broadcasted_iota(jnp.int32, (n, slot_count), 1)
-    chosen = jnp.where(slot_index < send_count[0][:, None], send_rows[0], -1)
-    halo = exchange_gather(n, chosen.reshape(slots, 1), features, slot_count)
+    halo = exchange_gather(n, send_count, send_rows.reshape(slots, 1), features, slot_count)
     blocks = lambda a: a.reshape(-1, edge, width)
     activation, own_grad, halo_grad, weight_part, bias_part = local_pass(
         n, tile_row, tile_col, tile_count, blocks(features), blocks(halo), tile_values,
         blocks(cotangent), weight, bias_vector.reshape(1, width),
     )
     scale = float(rows * n) ** (-0.5)
-    returned, weight_sum, bias_sum = exchange_return(
-        n, scale, halo_grad.reshape(n, slot_count, width), weight_part, bias_part
-    )
-    grad_features = scatter_add(
-        chosen.reshape(1, slots), returned.reshape(slots, width), own_grad.reshape(rows, width)
+    grad_features, weight_sum, bias_sum = exchange_return(
+        n, scale, send_count, send_rows.reshape(1, slots),
+        halo_grad.reshape(n, slot_count, width), weight_part, bias_part,
+        own_grad.reshape(rows, width),
     )
     return (activation.reshape(rows, width), grad_features, weight_sum, bias_sum.reshape(width))
 

time: 75.9 us -> 73.3 us (0.966); the launches traced: 75 us -> 73.2 us
  local copies, waits for them, and re-layouts: 2.56 us -> 6.66 us
  Pallas kernels: 69.1 us -> 65.3 us
  other arithmetic: 2.06 us -> 0 us
    pallas_call x1 -> x0, Pallas kernels: 4.7 us -> none  [scatter_add(): pl.pallas_call(scatter_kernel, out_shape=jax.ShapeDtypeStruct(own_grad.sh...]
    unnamed x7 -> x8, local copies, waits for them, and re-layouts: 2.05 us -> 5.13 us
    pallas_call x1, Pallas kernels: 33.2 us -> 30.8 us  [exchange_return(): pl.pallas_call(functools.partial(return_kernel, n, scale), out_shape=(jax...]
    pallas_call x1, Pallas kernels: 16.5 us -> 18.6 us  [local_pass(): pl.pallas_call(local_kernel, out_shape=(jax.ShapeDtypeStruct(features.sha...]
    reshape x0 -> x2, local copies, waits for them, and re-layouts: none -> 1.53 us  [the longest x1 0.86 us: body(): send_rows.reshape(slots, 1)]
    select_n x2 -> x0, other arithmetic: 1.33 us -> none  [body(): chosen = jnp.where(slot_index < send_count[0][:, None], send_rows[0], -1)]
    pallas_call x1, Pallas kernels: 14.7 us -> 15.9 us  [exchange_gather(): pl.pallas_call(functools.partial(gather_kernel, n), out_shape=jax.ShapeDt...]
where the time goes in v2:
time: 73.3 us; the launch traced here: 73.2 us
  Pallas kernels  65.3 us (89%)
  local copies, waits for them, and re-layouts  6.66 us (9%)
  between operations  1.32 us (2%)
    pallas_call x1, Pallas kernels, exchange_return(): pl.pallas_call(functools.partial(return_kernel, n, scale), out_shape=(jax...  30.8 us
    pallas_call x1, Pallas kernels, local_pass(): pl.pallas_call(local_kernel, out_shape=(jax.ShapeDtypeStruct(features.sha...  18.6 us
    pallas_call x1, Pallas kernels, exchange_gather(): pl.pallas_call(functools.partial(gather_kernel, n), out_shape=jax.ShapeDt...  15.9 us
    unnamed x8, local copies, waits for them, and re-layouts  5.13 us

profile of v2, /device:TPU:0, one launch (start us, length us, event | category | flops | bytes accessed | tf_op | source)
XLA Modules:
  0.0 73.2 jit_solution(14751319508286815776)
XLA Ops:
  1.3 0.8 %copy.16 = s32[1,32,16]{2,1,0:T(8,128)S(1)} copy(s32[1,32,16]{1,2,0:T(8,128)} %param.17) | data formatting | bytes 4096 | tf_op args[7]
  2.0 0.7 reshape.44.chosen_ref
  2.7 0.9 %reshape.48.chosen_ref = s32[512,1]{1,0:T(8,128)} reshape(s32[1,32,16]{2,1,0:T(8,128)S(1)} %copy.16) | data formatting | bytes 4096 | tf_op jit(solution)/shard_map/reshape | solution.py:403
  3.6 15.9 %gather_exchange.1 = bf16[32,16,256]{2,1,0:T(8,128)(2,1)} custom-call(s32[1,32]{1,0:T(1,128)} %count_ref.3, s32[512,1]{1,0:T(8,128)} %reshape.48.chosen_ref, bf16[4096,256]{1,0:T(8,128)(2,1)} %features_hbm.1), custom_call_target="tpu_custom_call" | custom-call | flops 1073741824 | bytes 16777216 | tf_op jit(solution)/shard_map/gather_exchange/pallas_call | solution.py:97
  19.5 18.6 %local_pass.1 = (bf16[32,128,256]{2,1,0:T(8,128)(2,1)}, bf16[32,128,256]{2,1,0:T(8,128)(2,1)}, bf16[4,128,256]{2,1,0:T(8,128)(2,1)}, bf16[32,8,256]{2,1,0:T(8,128)(2,1)}, f32[1,256]{1,0:T(1,128)}) custom-call(s32[1,256]{1,0:T(1,128)} %tile_row.1, s32[1,256]{1,0:T(1,128)} %tile_col.1, s32[1]{0:T(128)S(6)} %copy.22.tile_count, bf16[32,128,256]{2,1,0:T(8,128)(2,1)} %bitcast.9, ...), custom_call_target="tpu_custom_call" | custom-call | tf_op jit(solution)/shard_map/local_pass/pallas_call | solution.py:257
  38.1 30.8 %return_exchange.1 = (bf16[4096,256]{1,0:T(8,128)(2,1)}, f32[256,256]{1,0:T(8,128)}, f32[1,256]{1,0:T(1,128)}) custom-call(s32[1,32]{1,0:T(1,128)} %count_ref.3, s32[1,512]{1,0:T(1,128)} %reshape.44.chosen_ref, bf16[32,16,256]{2,1,0:T(8,128)(2,1)} %bitcast.11, bf16[32,8,256]{2,1,0:T(8,128)(2,1)} %get-tuple-element.14.weight_ref, ...), custom_call_target="tpu_custom_call" | custom-call | tf_op jit(solution)/shard_map/return_exchange/pallas_call | solution.py:363
  68.9 0.0 copy-start
  68.9 0.0 copy-start.1
  68.9 3.1 %copy.23 = bf16[4096,256]{1,0:T(8,128)(2,1)} copy(bf16[4096,256]{1,0:T(8,128)(2,1)} %get-tuple-element.25) | data formatting | bytes 4194304
  72.0 0.0 copy-done
  72.0 0.7 copy.24
  72.7 0.0 copy-done.1
  72.7 0.6 copy.25
Async XLA Ops:
  68.9 3.1 %copy-start = (f32[256,256]{1,0:T(8,128)S(1)}, f32[256,256]{1,0:T(8,128)}, u32[]{:S(2)}) copy-start(f32[256,256]{1,0:T(8,128)} %get-tuple-element.26) | copy-start | bytes 786436
  68.9 3.8 %copy-start.1 = (f32[1,256]{1,0:T(1,128)S(1)}, f32[1,256]{1,0:T(1,128)}, u32[]{:S(2)}) copy-start(f32[1,256]{1,0:T(1,128)} %get-tuple-element.19) | copy-start | bytes 3076
